TPU v7x, 128 devices: a whole 4x4x4 slice. The times are simulated.
128 devices in a mesh: blk: 64 (over z_lo, x, y, core), grp: 2 (over z_hi).
Axes of the slice: x: 4, y: 4, z: 4 (z_hi: 2, z_lo: 2; z = z_hi * 2 + z_lo), core: 2. Of those that a mesh axis runs over, the one named last changes fastest.
Arguments:
- returns: float32 [512, 32768], P(None, ('blk', 'grp')), may hold values from -200 to 200
Outputs:
- correlation: bfloat16 [32768, 32768], P(('blk', 'grp'))
All inputs are finite; a program needn't handle non-finite values.
Results may differ from a plain program's by a relative error of at most 0.0034.
Values may be sent and summed in bfloat16 or wider, within the bound.
A program may use at most 128 MiB of HBM per device.

v0:
```python
import math
import jax
import jax.numpy as jnp
from jax import lax
from jax.sharding import Mesh
from jax.sharding import PartitionSpec as P

BLK_GRP = ("blk_0", "blk_1", "blk_2", "blk_3", "grp")


def by_axis(array, axes):
    for axis in axes:
        array = lax.psum(array, axis)
    return array


def gram_tile(first, second):
    return lax.dot_general(
        first, second, (((0,), (0,)), ((), ())), preferred_element_type=jnp.float32
    )


def shards(returns):
    bar_count = returns.shape[0]
    series_dev = returns.shape[1]
    devices = lax.axis_size(BLK_GRP)
    my_index = lax.axis_index(BLK_GRP)
    summed = by_axis(jnp.sum(returns, axis=1), BLK_GRP)
    market = summed / (series_dev * devices)
    excess = returns - market[:, None]
    deviation = excess - jnp.mean(excess, axis=0, keepdims=True)
    inverse = lax.rsqrt(jnp.mean(deviation * deviation, axis=0, keepdims=True) + 1e-06) / math.sqrt(
        bar_count
    )
    zscores = (deviation * inverse).astype(jnp.bfloat16)
    piece = lax.all_gather(zscores, BLK_GRP, axis=1, tiled=True)
    products = gram_tile(zscores, piece)
    column_block = jnp.arange(piece.shape[1], dtype=jnp.int32) // series_dev
    return jnp.where(column_block[None, :] >= my_index, products, jnp.float32(0.0)).astype(
        jnp.bfloat16
    )


def solution(mesh):
    split = Mesh(
        mesh.devices.reshape(2, 4, 4, 2, mesh.shape["grp"]),
        ("blk_0", "blk_1", "blk_2", "blk_3", "grp"),
    )
    in_specs = (P(None, BLK_GRP),)
    out_specs = P(BLK_GRP, None)
    return jax.shard_map(
        shards, mesh=split, in_specs=in_specs, out_specs=out_specs, check_vma=False
    )
```

profile of v0, /device:TPU:1, one launch (start us, length us, event | category | flops | bytes accessed | tf_op | source)
XLA Modules:
  0.0 429.9 jit_solution(4869989052520204716)
XLA Ops:
  6.5 0.0 all-gather.2.cloned.1.call-start
  6.5 1.2 reduce_sum.27
  7.7 4.8 %psum.35 = f32[512]{0:T(512)S(1)} all-reduce(f32[512]{0:T(512)S(1)} %reduce_sum.27), channel_id=1, replica_groups=mesh['blk_0'=2,'blk_1'=4,'blk_2'=4,'blk_3'=2,'grp'=2] {'blk_0'}, use_global_device_ids=true, to_apply=%region_1.0 | all-reduce | flops 512 | bytes 4096 | tf_op jit(solution)/shard_map/psum | solution.py:13
  12.5 8.4 %psum.36 = f32[512]{0:T(512)S(1)} all-reduce(f32[512]{0:T(512)S(1)} %psum.35), channel_id=1, replica_groups=mesh['blk_0'=2,'blk_1'=4,'blk_2'=4,'blk_3'=2,'grp'=2] {'blk_1'}, use_global_device_ids=true, to_apply=%region_2.0 | all-reduce | flops 512 | bytes 4096 | tf_op jit(solution)/shard_map/psum | solution.py:13
  20.9 8.7 %psum.37 = f32[512]{0:T(512)S(1)} all-reduce(f32[512]{0:T(512)S(1)} %psum.36), channel_id=1, replica_groups=mesh['blk_0'=2,'blk_1'=4,'blk_2'=4,'blk_3'=2,'grp'=2] {'blk_2'}, use_global_device_ids=true, to_apply=%region_3.0 | all-reduce | flops 512 | bytes 4096 | tf_op jit(solution)/shard_map/psum | solution.py:13
  29.6 7.8 %psum.38 = f32[512]{0:T(512)S(1)} all-reduce(f32[512]{0:T(512)S(1)} %psum.37), channel_id=1, replica_groups=mesh['blk_0'=2,'blk_1'=4,'blk_2'=4,'blk_3'=2,'grp'=2] {'blk_3'}, use_global_device_ids=true, to_apply=%region_4.0 | all-reduce | flops 512 | bytes 4096 | tf_op jit(solution)/shard_map/psum | solution.py:13
  37.4 5.9 %psum.39 = f32[512]{0:T(512)S(1)} all-reduce(f32[512]{0:T(512)S(1)} %psum.38), channel_id=1, replica_groups=mesh['blk_0'=2,'blk_1'=4,'blk_2'=4,'blk_3'=2,'grp'=2] {'grp'}, use_global_device_ids=true, to_apply=%region_5.0 | all-reduce | flops 512 | bytes 4096 | tf_op jit(solution)/shard_map/psum | solution.py:13
  43.3 1.2 subtract_reduce_fusion
  44.5 1.2 multiply_reduce_fusion
  45.7 1.9 multiply_convert_fusion
  47.6 0.0 all-gather.2.cloned.1.call-update
  47.7 354.2 %all-gather.2.cloned.1.call-done = bf16[512,32768]{1,0:T(8,128)(2,1)} async-done(((bf16[512,256]{1,0:T(8,128)(2,1)}), bf16[512,32768]{1,0:T(8,128)(2,1)}) %all-gather.2.cloned.1.call-update) | async-done | bytes 33554448 | tf_op jit(solution)/shard_map/all_gather | solution.py:36
  401.9 21.2 %fusion = bf16[256,32768]{1,0:T(8,128)(2,1)} fusion(bf16[512,256]{1,0:T(8,128)(2,1)} %multiply_convert_fusion, bf16[512,32768]{1,0:T(8,128)(2,1)} %all-gather.2.cloned.1.call-done, pred[32768]{0:T(1024)(128)(4,1)S(1)} %fusion.1), kind=kOutput, calls=%fused_computation.1 | convolution fusion | flops 8606711808 | bytes 50626560 | tf_op jit(solution)/shard_map/dot_general | solution.py:18
  (4 shorter events, 0.1 us)
Async XLA Ops:
  6.5 395.3 %all-gather.2.cloned.1.call-start = ((), (), s32[]{:S(2)}) async-start(), calls=%async_computation | async-start | bytes 33816576 | tf_op jit(solution)/shard_map/all_gather | solution.py:36
Sparse Core Ops, SparseCore 0:
  47.8 354.0 all-gather.1
where the time goes:
time: 430 us
  waiting for transfers between devices  354 us (82%)
  blocking collectives  35.6 us (8%)
  matrix products  21.2 us (5%)
  between operations  13.4 us (3%)
  other arithmetic  5.51 us (1%)
    all_gather x1, waiting for transfers between devices, shards(): piece = lax.all_gather(zscores, BLK_GRP, axis=1, tiled=True)  354 us
    psum x5, blocking collectives, by_axis(): array = lax.psum(array, axis)  35.6 us
    dot_general x1, matrix products, gram_tile(): lax.dot_general(first, second, (((0,), (0,)), ((), ())), preferred_elemen...  21.2 us
  transfers between devices with their start and end apart: 1, of which 1 were waited for; matrix products, arithmetic and copies ran while one was open for 0% of the time, Pallas kernels for 0%

commit v1 on v0

--- a/solution.py
+++ b/solution.py
@@ -33,7 +33,7 @@
         bar_count
     )
     zscores = (deviation * inverse).astype(jnp.bfloat16)
-    piece = lax.all_gather(zscores, BLK_GRP, axis=1, tiled=True)
+    piece = jnp.concatenate(lax.all_gather(zscores, BLK_GRP), axis=1)
     products = gram_tile(zscores, piece)
     column_block = jnp.arange(piece.shape[1], dtype=jnp.int32) // series_dev
     return jnp.where(column_block[None, :] >= my_index, products, jnp.float32(0.0)).astype(

time: 430 us -> 460 us (1.070)
  local copies, waits for them, and re-layouts: 0 us -> 44.1 us
  waiting for transfers between devices: 354 us -> 341 us
    reshape x0 -> x1, local copies, waits for them, and re-layouts: none -> 44.1 us  [shards(): piece = jnp.concatenate(lax.all_gather(zscores, BLK_GRP), axis=1)]
    all_gather x1, waiting for transfers between devices: 354 us -> 341 us  [shards(): piece = jnp.concatenate(lax.all_gather(zscores, BLK_GRP), axis=1)]
where the time goes in v1:
time: 460 us; the launch traced here: 459 us
  waiting for transfers between devices  341 us (74%)
  local copies, waits for them, and re-layouts  44.1 us (10%)
  blocking collectives  35.6 us (8%)
  matrix products  19.1 us (4%)
  between operations  13.4 us (3%)
  other arithmetic  5.51 us (1%)
    all_gather x1, waiting for transfers between devices, shards(): piece = jnp.concatenate(lax.all_gather(zscores, BLK_GRP), axis=1)  341 us
    reshape x1, local copies, waits for them, and re-layouts, shards(): piece = jnp.concatenate(lax.all_gather(zscores, BLK_GRP), axis=1)  44.1 us
    psum x5, blocking collectives, by_axis(): array = lax.psum(array, axis)  35.6 us
    dot_general x1, matrix products, gram_tile(): lax.dot_general(first, second, (((0,), (0,)), ((), ())), preferred_elemen...  19.1 us
  transfers between devices with their start and end apart: 1, of which 1 were waited for; matrix products, arithmetic and copies ran while one was open for 0% of the time, Pallas kernels for 0%

profile of v1, /device:TPU:1, one launch (start us, length us, event | category | flops | bytes accessed | tf_op | source)
XLA Modules:
  0.0 458.8 jit_solution(12013001140041439618)
XLA Ops:
  6.5 0.0 all-gather.3.cloned.1.call-start
  6.5 1.2 reduce_sum.27
  7.7 4.8 %psum.35 = f32[512]{0:T(512)S(1)} all-reduce(f32[512]{0:T(512)S(1)} %reduce_sum.27), channel_id=1, replica_groups=mesh['blk_0'=2,'blk_1'=4,'blk_2'=4,'blk_3'=2,'grp'=2] {'blk_0'}, use_global_device_ids=true, to_apply=%region_1.0 | all-reduce | flops 512 | bytes 4096 | tf_op jit(solution)/shard_map/psum | solution.py:13
  12.5 8.4 %psum.36 = f32[512]{0:T(512)S(1)} all-reduce(f32[512]{0:T(512)S(1)} %psum.35), channel_id=1, replica_groups=mesh['blk_0'=2,'blk_1'=4,'blk_2'=4,'blk_3'=2,'grp'=2] {'blk_1'}, use_global_device_ids=true, to_apply=%region_2.0 | all-reduce | flops 512 | bytes 4096 | tf_op jit(solution)/shard_map/psum | solution.py:13
  20.9 8.7 %psum.37 = f32[512]{0:T(512)S(1)} all-reduce(f32[512]{0:T(512)S(1)} %psum.36), channel_id=1, replica_groups=mesh['blk_0'=2,'blk_1'=4,'blk_2'=4,'blk_3'=2,'grp'=2] {'blk_2'}, use_global_device_ids=true, to_apply=%region_3.0 | all-reduce | flops 512 | bytes 4096 | tf_op jit(solution)/shard_map/psum | solution.py:13
  29.6 7.8 %psum.38 = f32[512]{0:T(512)S(1)} all-reduce(f32[512]{0:T(512)S(1)} %psum.37), channel_id=1, replica_groups=mesh['blk_0'=2,'blk_1'=4,'blk_2'=4,'blk_3'=2,'grp'=2] {'blk_3'}, use_global_device_ids=true, to_apply=%region_4.0 | all-reduce | flops 512 | bytes 4096 | tf_op jit(solution)/shard_map/psum | solution.py:13
  37.4 5.9 %psum.39 = f32[512]{0:T(512)S(1)} all-reduce(f32[512]{0:T(512)S(1)} %psum.38), channel_id=1, replica_groups=mesh['blk_0'=2,'blk_1'=4,'blk_2'=4,'blk_3'=2,'grp'=2] {'grp'}, use_global_device_ids=true, to_apply=%region_5.0 | all-reduce | flops 512 | bytes 4096 | tf_op jit(solution)/shard_map/psum | solution.py:13
  43.3 1.2 subtract_reduce_fusion
  44.5 1.2 multiply_reduce_fusion
  45.7 1.9 multiply_convert_fusion
  47.6 0.0 all-gather.3.cloned.1.call-update
  47.7 341.1 %all-gather.3.cloned.1.call-done = bf16[65536,256]{1,0:T(8,128)(2,1)} async-done(((bf16[512,256]{1,0:T(8,128)(2,1)}), bf16[65536,256]{1,0:T(8,128)(2,1)}) %all-gather.3.cloned.1.call-update) | async-done | bytes 33554448 | tf_op jit(solution)/shard_map/all_gather | solution.py:36
  388.8 0.0 copy-start
  388.8 44.1 %copy.2 = bf16[512,128,256]{0,2,1:T(8,128)(2,1)} copy(bf16[512,128,256]{2,0,1:T(8,128)(2,1)} %bitcast.6) | data formatting | bytes 67108864 | tf_op jit(solution)/shard_map/reshape | solution.py:36
  432.9 0.0 copy-done
  432.9 19.1 %fusion = bf16[256,32768]{1,0:T(8,128)(2,1)} fusion(bf16[512,256]{1,0:T(8,128)(2,1)S(1)} %copy-done, bf16[512,32768]{0,1:T(8,128)(2,1)} %bitcast.7, pred[32768]{0:T(1024)(128)(4,1)S(1)} %fusion.1), kind=kOutput, calls=%fused_computation.1 | convolution fusion | flops 8606711808 | bytes 50626560 | tf_op jit(solution)/shard_map/dot_general | solution.py:18
  (4 shorter events, 0.1 us)
Async XLA Ops:
  6.5 382.3 %all-gather.3.cloned.1.call-start = ((), (), s32[]{:S(2)}) async-start(), calls=%async_computation | async-start | bytes 33816576 | tf_op jit(solution)/shard_map/all_gather | solution.py:36
  388.8 44.1 %copy-start = (bf16[512,256]{1,0:T(8,128)(2,1)S(1)}, bf16[512,256]{1,0:T(8,128)(2,1)}, u32[]{:S(2)}) copy-start(bf16[512,256]{1,0:T(8,128)(2,1)} %multiply_convert_fusion) | copy-start | bytes 786436
Sparse Core Ops, SparseCore 0:
  47.8 340.9 all-gather.2
